TPU v7x, 256 devices: a whole 4x4x8 slice. The times are simulated.
256 devices in a mesh: dp: 8 (over x, core), param: 32 (over y, z).
Axes of the slice: x: 4, y: 4, z: 8, core: 2. Of those that a mesh axis runs over, the one named last changes fastest.
Arguments:
- train_grads: bfloat16 [7168, 212992], P('dp', 'param'), as said below
- query_grads: bfloat16 [256, 212992], P('dp', 'param'), as said below
Outputs:
- scores: float32 [256, 7168], P('param', 'dp')
Inputs may be any that keep to these rules, and one draw needn't show every extreme that they name: `train_grads`: finite real values. `query_grads`: finite real values.
All inputs are finite; a program needn't handle non-finite values.
Results may differ from a plain program's by a relative error of at most 0.0003.
Values may be sent and summed in bfloat16 or wider, within the bound.
A program may use at most 64 MiB of HBM per device.

v0:
```python
import jax
import jax.numpy as jnp
from jax import lax
from jax.sharding import PartitionSpec as P

epsilon = 1e-06


def in_blocks(x, dim, devices):
    lengths = x.shape
    pieces = x.reshape(*lengths[:dim], devices, lengths[dim] // devices, *lengths[dim + 1 :])
    return jnp.moveaxis(pieces, dim, 0)


def summed_on_arrival(x, axis, dim):
    devices = lax.axis_size(axis)
    pieces = lax.all_to_all(in_blocks(x, dim, devices), axis, 0, 0, tiled=True)
    return jnp.sum(pieces, axis=0)


def side_by_side(arrays, axis, dim, along):
    columns = [a.reshape(*a.shape[:along], -1) for a in arrays]
    both = jnp.concatenate(columns, axis=along)
    out, at, done = (summed_on_arrival(both, axis, dim), 0, [])
    for a, column in zip(arrays, columns):
        slab = out[..., at : at + column.shape[along]]
        done.append(slab.reshape(*slab.shape[:along], *a.shape[along:]))
        at += column.shape[along]
    return tuple(done)


def copy_for_each(x, axis):
    devices = lax.axis_size(axis)
    return lax.all_to_all(jnp.broadcast_to(x[None], (devices, *x.shape)), axis, 0, 0, tiled=True)


def taken_together(x, axis):
    everything = copy_for_each(x, axis)
    return jnp.sum(everything, axis=0)


def per_device(train_grads, query_grads):
    queries = lax.all_gather(query_grads, "dp", axis=0, tiled=True)
    products = lax.dot_general(
        queries, train_grads, (((1,), (1,)), ((), ())), preferred_element_type=jnp.float32
    )
    query_norm = jnp.sum(jnp.square(queries.astype(jnp.float32)), axis=1)
    train_norm = jnp.sum(jnp.square(train_grads.astype(jnp.float32)), axis=1)
    products, query_norm = side_by_side((products, query_norm), "param", 0, 1)
    train_norm = taken_together(train_norm, "param")
    return (
        products
        * lax.rsqrt(query_norm + epsilon)[:, None]
        * lax.rsqrt(train_norm + epsilon)[None, :]
    )


def solution(mesh):
    return jax.shard_map(
        per_device,
        mesh=mesh,
        in_specs=(P("dp", "param"), P("dp", "param")),
        out_specs=P("param", "dp"),
        check_vma=False,
    )
```

profile of v0, /device:TPU:32, one launch (start us, length us, event | category | flops | bytes accessed | tf_op | source)
XLA Modules:
  0.0 102.4 jit_solution(12826004121880036399)
XLA Ops:
  6.5 0.0 all-gather.2.cloned.1.call-start
  6.5 0.7 all-gather.2.cloned.1.call-update
  7.3 6.8 %multiply_reduce_fusion = f32[896]{0:T(1024)S(1)} fusion(bf16[896,6656]{1,0:T(8,128)(2,1)} %param.2), kind=kLoop, calls=%fused_computation | loop fusion | flops 17890432 | bytes 11931136 | tf_op jit(solution)/shard_map/reduce_sum | solution.py:48
  14.0 0.7 broadcast_in_dim.2
  14.7 11.4 %all-to-all-start.1 = ((f32[32,1,896]{2,1,0:T(1,128)}), f32[32,1,896]{2,1,0:T(1,128)S(1)}, u32[]{:S(2)}, u32[]{:S(2)}) async-start(f32[32,1,896]{2,1,0:T(1,128)} %broadcast_in_dim.2), calls=%async_computation.1 | async-start | bytes 229376 | tf_op jit(solution)/shard_map/all_to_all | solution.py:34
  26.1 17.0 %all-gather.2.cloned.1.call-done = bf16[256,6656]{1,0:T(8,128)(2,1)} async-done(((bf16[32,6656]{1,0:T(8,128)(2,1)}), bf16[256,6656]{1,0:T(8,128)(2,1)}) %all-gather.2.cloned.1.call-update) | async-done | bytes 3407888 | tf_op jit(solution)/shard_map/all_gather | solution.py:43
  43.1 0.0 copy-start
  43.1 10.6 %convolution_bitcast_fusion = f32[32,8,896]{2,1,0:T(8,128)S(1)} fusion(bf16[256,6656]{1,0:T(8,128)(2,1)} %all-gather.2.cloned.1.call-done, bf16[896,6656]{1,0:T(8,128)(2,1)} %param.2), kind=kOutput, calls=%fused_computation.2 | convolution fusion | flops 3053453312 | bytes 16252928 | tf_op jit(solution)/shard_map/dot_general | solution.py:44
  53.8 0.0 copy-done
  53.8 0.8 multiply_reduce_fusion.1
  54.5 0.2 concatenate.11
  54.7 1.1 %pad_maximum_fusion = f32[32,8,897]{2,1,0:T(8,128)} fusion(f32[32,8,1]{2,1,0:T(8,128)S(1)} %concatenate.11, f32[32,8,896]{2,1,0:T(8,128)S(1)} %convolution_bitcast_fusion), kind=kLoop, calls=%fused_computation.3 | loop fusion | flops 229632 | bytes 1837056 | tf_op jit(solution)/shard_map/concatenate | solution.py:23
  55.8 0.0 all-to-all-done.1
  55.9 10.1 %all-to-all-start = ((f32[32,8,897]{2,1,0:T(8,128)}), f32[32,8,897]{2,1,0:T(8,128)S(1)}, u32[]{:S(2)}, u32[]{:S(2)}) async-start(f32[32,8,897]{2,1,0:T(8,128)} %pad_maximum_fusion), calls=%async_computation | async-start | bytes 2097152 | tf_op jit(solution)/shard_map/all_to_all | solution.py:17
  65.9 0.1 reduce_sum.39
  66.0 28.6 %all-to-all-done = f32[32,8,897]{2,1,0:T(8,128)S(1)} async-done(((f32[32,8,897]{2,1,0:T(8,128)}), f32[32,8,897]{2,1,0:T(8,128)S(1)}, u32[]{:S(2)}, u32[]{:S(2)}) %all-to-all-start) | async-done | bytes 918560 | tf_op jit(solution)/shard_map/all_to_all | solution.py:17
  94.7 0.1 reduce_sum.37
  94.7 0.1 fusion.2
  94.9 0.7 fusion
  (1 shorter events, 0.0 us)
Async XLA Ops:
  6.5 36.6 %all-gather.2.cloned.1.call-start = ((), (), s32[]{:S(2)}) async-start(), calls=%async_computation.2 | async-start | bytes 3833856 | tf_op jit(solution)/shard_map/all_gather | solution.py:43
  14.7 41.1 %all-to-all-start.1 = ((f32[32,1,896]{2,1,0:T(1,128)}), f32[32,1,896]{2,1,0:T(1,128)S(1)}, u32[]{:S(2)}, u32[]{:S(2)}) async-start(f32[32,1,896]{2,1,0:T(1,128)} %broadcast_in_dim.2), calls=%async_computation.1 | async-start | bytes 229376 | tf_op jit(solution)/shard_map/all_to_all | solution.py:34
  43.1 10.7 %copy-start = (bf16[256,6656]{1,0:T(8,128)(2,1)S(1)}, bf16[256,6656]{1,0:T(8,128)(2,1)}, u32[]{:S(2)}) copy-start(bf16[256,6656]{1,0:T(8,128)(2,1)} %all-gather.2.cloned.1.call-done) | copy-start | bytes 10223620
  55.9 38.8 %all-to-all-start = ((f32[32,8,897]{2,1,0:T(8,128)}), f32[32,8,897]{2,1,0:T(8,128)S(1)}, u32[]{:S(2)}, u32[]{:S(2)}) async-start(f32[32,8,897]{2,1,0:T(8,128)} %pad_maximum_fusion), calls=%async_computation | async-start | bytes 2097152 | tf_op jit(solution)/shard_map/all_to_all | solution.py:17
Sparse Core Ops, SparseCore 0:
  9.2 33.8 all-gather.1
where the time goes:
time: 103 us; the launch traced here: 102 us
  waiting for transfers between devices  46.3 us (45%)
  starting transfers between devices  21.4 us (21%)
  between operations  13.4 us (13%)
  matrix products  10.6 us (10%)
  other arithmetic  9.61 us (9%)
    all_to_all x1, waiting for transfers between devices, summed_on_arrival(): pieces = lax.all_to_all(in_blocks(x, dim, devices), axis, 0, 0, tiled=True)  28.6 us
    all_gather x1, waiting for transfers between devices, per_device(): queries = lax.all_gather(query_grads, 'dp', axis=0, tiled=True)  17 us
    all_to_all x1, starting transfers between devices, copy_for_each(): lax.all_to_all(jnp.broadcast_to(x[None], (devices, *x.shape)), axis, 0, 0...  11.4 us
    dot_general x1, matrix products, per_device(): lax.dot_general(queries, train_grads, (((1,), (1,)), ((), ())), preferred...  10.6 us
    all_to_all x1, starting transfers between devices, summed_on_arrival(): pieces = lax.all_to_all(in_blocks(x, dim, devices), axis, 0, 0, tiled=True)  10.1 us
    reduce_sum x1, other arithmetic, per_device(): train_norm = jnp.sum(jnp.square(train_grads.astype(jnp.float32)), axis=1)  6.77 us
  transfers between devices with their start and end apart: 3, of which 2 were waited for; matrix products, arithmetic and copies ran while one was open for 20% of the time, Pallas kernels for 0%

commit v1 on v0

--- a/solution.py
+++ b/solution.py
@@ -4,6 +4,19 @@
 from jax.sharding import PartitionSpec as P
 
 epsilon = 1e-06
+
+
+def gather_around(shard, axis, dim):
+    ways = lax.axis_size(axis)
+    up = [(d, (d + 1) % ways) for d in range(ways)]
+    down = [(d, (d - 1) % ways) for d in range(ways)]
+    earlier, later = ([shard], [shard])
+    for _ in range(ways // 2):
+        earlier.append(lax.ppermute(earlier[-1], axis, up))
+    for _ in range((ways - 1) // 2):
+        later.append(lax.ppermute(later[-1], axis, down))
+    line = jnp.concatenate([*earlier[::-1], *later[1:]], axis=dim)
+    return jnp.roll(line, (lax.axis_index(axis) - ways // 2) * shard.shape[dim], axis=dim)
 
 
 def in_blocks(x, dim, devices):
@@ -40,7 +53,7 @@
 
 
 def per_device(train_grads, query_grads):
-    queries = lax.all_gather(query_grads, "dp", axis=0, tiled=True)
+    queries = gather_around(query_grads, "dp", 0)
     products = lax.dot_general(
         queries, train_grads, (((1,), (1,)), ((), ())), preferred_element_type=jnp.float32
     )

time: 103 us -> 122 us (1.18)
  local copies, waits for them, and re-layouts: 0.93 us -> 25.2 us
  between operations: 13.4 us -> 0.09 us
  starting transfers between devices: 21.4 us -> 29.5 us
  matrix products: 10.6 us -> 6.6 us
  other arithmetic: 9.61 us -> 12.7 us
    unnamed x2 -> x21, local copies, waits for them, and re-layouts: 0.01 us -> 23.5 us
    ppermute x0 -> x7, waiting for transfers between devices: none -> 20.7 us  [the longest x4 20.7 us: gather_around(): earlier.append(lax.ppermute(earlier[-1], axis, up))]
    all_gather x1 -> x0, waiting for transfers between devices: 17 us -> none  [per_device(): queries = lax.all_gather(query_grads, 'dp', axis=0, tiled=True)]
    ppermute x0 -> x7, starting transfers between devices: none -> 8.32 us  [the longest x3 8.31 us: gather_around(): later.append(lax.ppermute(later[-1], axis, down))]
    dot_general x1, matrix products: 10.6 us -> 6.6 us  [per_device(): lax.dot_general(queries, train_grads, (((1,), (1,)), ((), ())), preferred...]
    all_to_all x1, waiting for transfers between devices: 28.6 us -> 26.3 us  [summed_on_arrival(): pieces = lax.all_to_all(in_blocks(x, dim, devices), axis, 0, 0, tiled=True)]
    reduce_sum x1, other arithmetic: 0.76 us -> 2.72 us  [per_device(): query_norm = jnp.sum(jnp.square(queries.astype(jnp.float32)), axis=1)]
  transfers between devices with their start and end apart: 3 -> 9, of which waited for: 2 -> 4; matrix products, arithmetic and copies ran while one was open for 20% -> 35% of each run, Pallas kernels for 0% -> 0%
where the time goes in v1:
time: 122 us; the launch traced here: 121 us
  waiting for transfers between devices  47 us (39%)
  starting transfers between devices  29.5 us (24%)
  local copies, waits for them, and re-layouts  25.2 us (21%)
  other arithmetic  12.7 us (10%)
  matrix products  6.6 us (5%)
    all_to_all x1, waiting for transfers between devices, summed_on_arrival(): pieces = lax.all_to_all(in_blocks(x, dim, devices), axis, 0, 0, tiled=True)  26.3 us
    unnamed x21, local copies, waits for them, and re-layouts  23.5 us
    ppermute x4, waiting for transfers between devices, gather_around(): earlier.append(lax.ppermute(earlier[-1], axis, up))  20.7 us
    all_to_all x1, starting transfers between devices, copy_for_each(): lax.all_to_all(jnp.broadcast_to(x[None], (devices, *x.shape)), axis, 0, 0...  11.4 us
    all_to_all x1, starting transfers between devices, summed_on_arrival(): pieces = lax.all_to_all(in_blocks(x, dim, devices), axis, 0, 0, tiled=True)  9.78 us
    ppermute x3, starting transfers between devices, gather_around(): later.append(lax.ppermute(later[-1], axis, down))  8.31 us
    reduce_sum x1, other arithmetic, per_device(): train_norm = jnp.sum(jnp.square(train_grads.astype(jnp.float32)), axis=1)  6.77 us
    dot_general x1, matrix products, per_device(): lax.dot_general(queries, train_grads, (((1,), (1,)), ((), ())), preferred...  6.6 us
  transfers between devices with their start and end apart: 9, of which 4 were waited for; matrix products, arithmetic and copies ran while one was open for 35% of the time, Pallas kernels for 0%

profile of v1, /device:TPU:32, one launch (start us, length us, event | category | flops | bytes accessed | tf_op | source)
XLA Modules:
  0.0 121.1 jit_solution(9864693750480523951)
XLA Ops:
  0.0 0.0 collective-permute-start
  0.0 9.0 %collective-permute-done = bf16[32,6656]{1,0:T(8,128)(2,1)S(1)} collective-permute-done((bf16[32,6656]{1,0:T(8,128)(2,1)}, bf16[32,6656]{1,0:T(8,128)(2,1)S(1)}, u32[]{:S(2)}, u32[]{:S(2)}) %collective-permute-start) | collective-permute-done | bytes 426016 | tf_op jit(solution)/shard_map/ppermute | solution.py:15
  9.0 0.0 collective-permute-start.1
  9.0 3.0 %collective-permute-start.4 = (bf16[32,6656]{1,0:T(8,128)(2,1)}, bf16[32,6656]{1,0:T(8,128)(2,1)}, u32[]{:S(2)}, u32[]{:S(2)}) collective-permute-start(bf16[32,6656]{1,0:T(8,128)(2,1)} %param.3), channel_id=1, source_target_pairs={{0,224},{32,0},{64,32},{96,64},{128,96},{160,128},{192,160},{224,1... | collective-permute-start | bytes 1277960 | tf_op jit(solution)/shard_map/ppermute | solution.py:17
  11.9 5.8 %collective-permute-done.1 = bf16[32,6656]{1,0:T(8,128)(2,1)S(1)} collective-permute-done((bf16[32,6656]{1,0:T(8,128)(2,1)S(1)}, bf16[32,6656]{1,0:T(8,128)(2,1)S(1)}, u32[]{:S(2)}, u32[]{:S(2)}) %collective-permute-start.1) | collective-permute-done | bytes 426016 | tf_op jit(solution)/shard_map/ppermute | solution.py:15
  17.7 0.8 copy-done.2
  18.5 0.0 collective-permute-start.2
  18.5 0.0 collective-permute-done.4
  18.5 3.0 %collective-permute-start.5 = (bf16[32,6656]{1,0:T(8,128)(2,1)}, bf16[32,6656]{1,0:T(8,128)(2,1)}, u32[]{:S(2)}, u32[]{:S(2)}) collective-permute-start(bf16[32,6656]{1,0:T(8,128)(2,1)} %collective-permute-done.4), channel_id=1, source_target_pairs={{0,224},{32,0},{64,32},{96,64},{128,96},{160,128},{192,160},{224,1... | collective-permute-start | bytes 1277960 | tf_op jit(solution)/shard_map/ppermute | solution.py:17
  21.5 5.9 %collective-permute-done.2 = bf16[32,6656]{1,0:T(8,128)(2,1)} collective-permute-done((bf16[32,6656]{1,0:T(8,128)(2,1)S(1)}, bf16[32,6656]{1,0:T(8,128)(2,1)}, u32[]{:S(2)}, u32[]{:S(2)}) %collective-permute-start.2) | collective-permute-done | bytes 426016 | tf_op jit(solution)/shard_map/ppermute | solution.py:15
  27.4 0.0 collective-permute-start.3
  27.4 6.8 %multiply_reduce_fusion = f32[896]{0:T(1024)S(1)} fusion(bf16[896,6656]{1,0:T(8,128)(2,1)} %param.2), kind=kLoop, calls=%fused_computation | loop fusion | flops 17890432 | bytes 11931136 | tf_op jit(solution)/shard_map/reduce_sum | solution.py:61
  34.1 0.7 broadcast_in_dim.2
  34.9 11.4 %all-to-all-start.1 = ((f32[32,1,896]{2,1,0:T(1,128)}), f32[32,1,896]{2,1,0:T(1,128)S(1)}, u32[]{:S(2)}, u32[]{:S(2)}) async-start(f32[32,1,896]{2,1,0:T(1,128)} %broadcast_in_dim.2), calls=%async_computation.1 | async-start | bytes 229376 | tf_op jit(solution)/shard_map/all_to_all | solution.py:47
  46.2 0.0 copy-start
  46.3 0.0 collective-permute-done.5
  46.3 2.4 %collective-permute-start.6 = (bf16[32,6656]{1,0:T(8,128)(2,1)}, bf16[32,6656]{1,0:T(8,128)(2,1)S(1)}, u32[]{:S(2)}, u32[]{:S(2)}) collective-permute-start(bf16[32,6656]{1,0:T(8,128)(2,1)} %collective-permute-done.5), channel_id=1, source_target_pairs={{0,224},{32,0},{64,32},{96,64},{128,96},{160,128},{192,160},{224,1... | collective-permute-start | bytes 1277960 | tf_op jit(solution)/shard_map/ppermute | solution.py:17
  48.7 0.0 collective-permute-done.3
  48.7 2.5 %constant_dynamic-update-slice_fusion.15 = bf16[512,6656]{1,0:T(8,128)(2,1)} fusion(bf16[32,6656]{1,0:T(8,128)(2,1)} %collective-permute-done.3), kind=kLoop, calls=%fused_computation.21 | loop fusion | bytes 851968
  51.2 1.8 %constant_dynamic-update-slice_fusion.14 = bf16[512,6656]{1,0:T(8,128)(2,1)} fusion(bf16[512,6656]{1,0:T(8,128)(2,1)} %constant_dynamic-update-slice_fusion.15, bf16[32,6656]{1,0:T(8,128)(2,1)} %collective-permute-done.2), kind=kLoop, calls=%fused_computation.20 | loop fusion | bytes 851968
  53.0 1.8 %constant_dynamic-update-slice_fusion.13 = bf16[512,6656]{1,0:T(8,128)(2,1)} fusion(bf16[512,6656]{1,0:T(8,128)(2,1)} %constant_dynamic-update-slice_fusion.14, bf16[32,6656]{1,0:T(8,128)(2,1)} %copy-done.2), kind=kLoop, calls=%fused_computation.19 | loop fusion | bytes 851968
  54.8 0.8 constant_dynamic-update-slice_fusion.12
  55.6 0.0 copy-done.1
  55.6 0.8 constant_dynamic-update-slice_fusion.11
  56.4 1.8 %constant_dynamic-update-slice_fusion.10 = bf16[512,6656]{1,0:T(8,128)(2,1)} fusion(bf16[512,6656]{1,0:T(8,128)(2,1)} %constant_dynamic-update-slice_fusion.11, bf16[32,6656]{1,0:T(8,128)(2,1)} %collective-permute-done.4), kind=kLoop, calls=%fused_computation.16 | loop fusion | bytes 851968
  58.2 1.8 %constant_dynamic-update-slice_fusion.9 = bf16[512,6656]{1,0:T(8,128)(2,1)} fusion(bf16[512,6656]{1,0:T(8,128)(2,1)} %constant_dynamic-update-slice_fusion.10, bf16[32,6656]{1,0:T(8,128)(2,1)} %collective-permute-done.5), kind=kLoop, calls=%fused_computation.15 | loop fusion | bytes 851968
  60.0 0.0 collective-permute-done.6
  60.0 0.8 constant_dynamic-update-slice_fusion.8
  60.8 1.8 %constant_dynamic-update-slice_fusion.7 = bf16[512,6656]{1,0:T(8,128)(2,1)} fusion(bf16[512,6656]{1,0:T(8,128)(2,1)} %constant_dynamic-update-slice_fusion.8, bf16[32,6656]{1,0:T(8,128)(2,1)} %collective-permute-done.3), kind=kLoop, calls=%fused_computation.13 | loop fusion | bytes 851968
  62.6 1.8 %constant_dynamic-update-slice_fusion.6 = bf16[512,6656]{1,0:T(8,128)(2,1)} fusion(bf16[512,6656]{1,0:T(8,128)(2,1)} %constant_dynamic-update-slice_fusion.7, bf16[32,6656]{1,0:T(8,128)(2,1)} %collective-permute-done.2), kind=kLoop, calls=%fused_computation.12 | loop fusion | bytes 851968
  64.4 1.8 %constant_dynamic-update-slice_fusion.5 = bf16[512,6656]{1,0:T(8,128)(2,1)} fusion(bf16[512,6656]{1,0:T(8,128)(2,1)} %constant_dynamic-update-slice_fusion.6, bf16[32,6656]{1,0:T(8,128)(2,1)} %copy-done.2), kind=kLoop, calls=%fused_computation.11 | loop fusion | bytes 851968
  66.2 0.8 constant_dynamic-update-slice_fusion.4
  67.0 0.8 constant_dynamic-update-slice_fusion.3
  67.8 1.8 %constant_dynamic-update-slice_fusion.2 = bf16[512,6656]{1,0:T(8,128)(2,1)} fusion(bf16[512,6656]{1,0:T(8,128)(2,1)} %constant_dynamic-update-slice_fusion.3, bf16[32,6656]{1,0:T(8,128)(2,1)} %collective-permute-done.4), kind=kLoop, calls=%fused_computation.8 | loop fusion | bytes 851968
  69.6 1.8 %constant_dynamic-update-slice_fusion.1 = bf16[512,6656]{1,0:T(8,128)(2,1)} fusion(bf16[512,6656]{1,0:T(8,128)(2,1)} %constant_dynamic-update-slice_fusion.2, bf16[32,6656]{1,0:T(8,128)(2,1)} %collective-permute-done.5), kind=kLoop, calls=%fused_computation.7 | loop fusion | bytes 851968
  71.4 0.8 constant_dynamic-update-slice_fusion
  72.2 0.0 copy-done
  72.2 6.6 %fusion.2 = f32[32,8,896]{2,1,0:T(8,128)} fusion(bf16[896,6656]{1,0:T(8,128)(2,1)S(1)} %copy-done, bf16[512,6656]{1,0:T(8,128)(2,1)} %constant_dynamic-update-slice_fusion, s32[]{:T(128)S(6)} %select_n.14), kind=kOutput, calls=%fused_computation.4 | convolution fusion | flops 3053453312 | bytes 16252932 | tf_op jit(solution)/shard_map/dot_general | solution.py:57
  78.8 2.7 %multiply_reduce_fusion.1 = f32[256]{0:T(256)S(1)} fusion(bf16[512,6656]{1,0:T(8,128)(2,1)} %constant_dynamic-update-slice_fusion, s32[]{:T(128)S(6)} %select_n.14), kind=kLoop, calls=%fused_computation.1 | loop fusion | flops 5111552 | bytes 3408900 | tf_op jit(solution)/shard_map/reduce_sum | solution.py:60
  81.5 0.2 concatenate.18
  81.7 2.3 %pad_maximum_fusion = f32[32,8,897]{2,1,0:T(8,128)} fusion(f32[32,8,1]{2,1,0:T(8,128)S(1)} %concatenate.18, f32[32,8,896]{2,1,0:T(8,128)} %fusion.2), kind=kLoop, calls=%fused_computation.5 | loop fusion | flops 229632 | bytes 1837056 | tf_op jit(solution)/shard_map/concatenate | solution.py:36
  84.0 0.0 all-to-all-done.1
  84.0 9.8 %all-to-all-start = ((f32[32,8,897]{2,1,0:T(8,128)}), f32[32,8,897]{2,1,0:T(8,128)S(1)}, u32[]{:S(2)}, u32[]{:S(2)}) async-start(f32[32,8,897]{2,1,0:T(8,128)} %pad_maximum_fusion), calls=%async_computation | async-start | bytes 2097152 | tf_op jit(solution)/shard_map/all_to_all | solution.py:30
  93.8 0.1 reduce_sum.39
  93.9 26.3 %all-to-all-done = f32[32,8,897]{2,1,0:T(8,128)S(1)} async-done(((f32[32,8,897]{2,1,0:T(8,128)}), f32[32,8,897]{2,1,0:T(8,128)S(1)}, u32[]{:S(2)}, u32[]{:S(2)}) %all-to-all-start) | async-done | bytes 918560 | tf_op jit(solution)/shard_map/all_to_all | solution.py:30
  120.2 0.1 reduce_sum.37
  120.3 0.1 fusion.7
  120.4 0.7 fusion.5
  (3 shorter events, 0.0 us)
Async XLA Ops:
  0.0 55.6 %copy-start.1 = (bf16[32,6656]{1,0:T(8,128)(2,1)S(1)}, bf16[32,6656]{1,0:T(8,128)(2,1)}, u32[]{:S(2)}) copy-start(bf16[32,6656]{1,0:T(8,128)(2,1)} %param.3) | copy-start | bytes 1277956
  0.0 9.0 %collective-permute-start = (bf16[32,6656]{1,0:T(8,128)(2,1)}, bf16[32,6656]{1,0:T(8,128)(2,1)S(1)}, u32[]{:S(2)}, u32[]{:S(2)}) collective-permute-start(bf16[32,6656]{1,0:T(8,128)(2,1)} %param.3), channel_id=1, source_target_pairs={{0,32},{32,64},{64,96},{96,128},{128,160},{160,192},{192,224},{224... | collective-permute-start | bytes 1277960 | tf_op jit(solution)/shard_map/ppermute | solution.py:15
  9.0 8.8 %collective-permute-start.1 = (bf16[32,6656]{1,0:T(8,128)(2,1)S(1)}, bf16[32,6656]{1,0:T(8,128)(2,1)S(1)}, u32[]{:S(2)}, u32[]{:S(2)}) collective-permute-start(bf16[32,6656]{1,0:T(8,128)(2,1)S(1)} %collective-permute-done), channel_id=1, source_target_pairs={{0,32},{32,64},{64,96},{96,128},{128,160},{160,192},{192,224},{224... | collective-permute-start | bytes 1277960 | tf_op jit(solution)/shard_map/ppermute | solution.py:15
  9.0 9.5 %collective-permute-start.4 = (bf16[32,6656]{1,0:T(8,128)(2,1)}, bf16[32,6656]{1,0:T(8,128)(2,1)}, u32[]{:S(2)}, u32[]{:S(2)}) collective-permute-start(bf16[32,6656]{1,0:T(8,128)(2,1)} %param.3), channel_id=1, source_target_pairs={{0,224},{32,0},{64,32},{96,64},{128,96},{160,128},{192,160},{224,1... | collective-permute-start | bytes 1277960 | tf_op jit(solution)/shard_map/ppermute | solution.py:17
  17.7 0.8 copy-start.2
  18.5 8.9 %collective-permute-start.2 = (bf16[32,6656]{1,0:T(8,128)(2,1)S(1)}, bf16[32,6656]{1,0:T(8,128)(2,1)}, u32[]{:S(2)}, u32[]{:S(2)}) collective-permute-start(bf16[32,6656]{1,0:T(8,128)(2,1)S(1)} %collective-permute-done.1), channel_id=1, source_target_pairs={{0,32},{32,64},{64,96},{96,128},{128,160},{160,192},{192,224},{224... | collective-permute-start | bytes 1277960 | tf_op jit(solution)/shard_map/ppermute | solution.py:15
  18.5 27.8 %collective-permute-start.5 = (bf16[32,6656]{1,0:T(8,128)(2,1)}, bf16[32,6656]{1,0:T(8,128)(2,1)}, u32[]{:S(2)}, u32[]{:S(2)}) collective-permute-start(bf16[32,6656]{1,0:T(8,128)(2,1)} %collective-permute-done.4), channel_id=1, source_target_pairs={{0,224},{32,0},{64,32},{96,64},{128,96},{160,128},{192,160},{224,1... | collective-permute-start | bytes 1277960 | tf_op jit(solution)/shard_map/ppermute | solution.py:17
  27.4 21.3 %collective-permute-start.3 = (bf16[32,6656]{1,0:T(8,128)(2,1)}, bf16[32,6656]{1,0:T(8,128)(2,1)}, u32[]{:S(2)}, u32[]{:S(2)}) collective-permute-start(bf16[32,6656]{1,0:T(8,128)(2,1)} %collective-permute-done.2), channel_id=1, source_target_pairs={{0,32},{32,64},{64,96},{96,128},{128,160},{160,192},{192,224},{224... | collective-permute-start | bytes 1277960 | tf_op jit(solution)/shard_map/ppermute | solution.py:15
  34.9 49.1 %all-to-all-start.1 = ((f32[32,1,896]{2,1,0:T(1,128)}), f32[32,1,896]{2,1,0:T(1,128)S(1)}, u32[]{:S(2)}, u32[]{:S(2)}) async-start(f32[32,1,896]{2,1,0:T(1,128)} %broadcast_in_dim.2), calls=%async_computation.1 | async-start | bytes 229376 | tf_op jit(solution)/shard_map/all_to_all | solution.py:47
  46.2 25.9 %copy-start = (bf16[896,6656]{1,0:T(8,128)(2,1)S(1)}, bf16[896,6656]{1,0:T(8,128)(2,1)}, u32[]{:S(2)}) copy-start(bf16[896,6656]{1,0:T(8,128)(2,1)} %param.2) | copy-start | bytes 35782660
  46.3 13.7 %collective-permute-start.6 = (bf16[32,6656]{1,0:T(8,128)(2,1)}, bf16[32,6656]{1,0:T(8,128)(2,1)S(1)}, u32[]{:S(2)}, u32[]{:S(2)}) collective-permute-start(bf16[32,6656]{1,0:T(8,128)(2,1)} %collective-permute-done.5), channel_id=1, source_target_pairs={{0,224},{32,0},{64,32},{96,64},{128,96},{160,128},{192,160},{224,1... | collective-permute-start | bytes 1277960 | tf_op jit(solution)/shard_map/ppermute | solution.py:17
  84.0 36.2 %all-to-all-start = ((f32[32,8,897]{2,1,0:T(8,128)}), f32[32,8,897]{2,1,0:T(8,128)S(1)}, u32[]{:S(2)}, u32[]{:S(2)}) async-start(f32[32,8,897]{2,1,0:T(8,128)} %pad_maximum_fusion), calls=%async_computation | async-start | bytes 2097152 | tf_op jit(solution)/shard_map/all_to_all | solution.py:30
